TPU v7x, 32 devices: a whole 2x2x4 slice. The times are simulated.
32 devices in a mesh: dp: 4 (over x, core), section: 2 (over y), tensor: 4 (over z).
Axes of the slice: x: 2, y: 2, z: 4, core: 2. Of those that a mesh axis runs over, the one named last changes fastest.
Arguments:
- observed: float32 [4, 2, 4, 2646], P('dp', 'section', 'tensor'), may hold values from 0.25 to 8
- section_of: int32 [126], replicated, may hold values from 0 to 1, as said below
- hist_len: int32 [21], replicated, may hold values from 1 to 127
- roll_index: int32 [], replicated, may hold values from 0 to 127
- history: float32 [128, 2646], replicated, may hold values from 0.02 to 64
- acts: bfloat16 [2, 1536, 16384], P('section', 'dp', 'tensor'), may hold values from -6 to 6
- grads: bfloat16 [2, 1536, 1024], P('section', 'dp', 'tensor'), may hold values from -6 to 6
Outputs:
- new_history: float32 [128, 2646], replicated
- new_scale: float32 [2646], replicated
- wgrad: bfloat16 [2, 16384, 1024], P('section', ('tensor', 'dp'))
Inputs may be any that keep to these rules, and one draw needn't show every extreme that they name: `section_of`: layers are assigned to sections in contiguous ascending groups, and every section holds at least one layer.
All inputs are finite; a program needn't handle non-finite values.
Results may differ from a plain program's by a relative error of at most 0.017.
Values may be sent and summed in bfloat16 or wider, within the bound.
A program may use at most 64 MiB of HBM per device.

v0:
```python
import jax
import jax.numpy as jnp
from jax import lax
from jax.sharding import PartitionSpec as P

FP8_MAX = 448.0


def merge_amax(local):
    merged = lax.pmax(local, "tensor")
    merged = lax.pmax(merged, "section")
    return lax.pmax(merged, "dp")


def weight_grad(acts, grads, scale_x, scale_g):
    denom = scale_x * scale_g
    acts_q = jnp.clip(acts[0].astype(jnp.float32) * scale_x, -FP8_MAX, FP8_MAX).astype(jnp.bfloat16)
    grads_q = jnp.clip(grads[0].astype(jnp.float32) * scale_g, -FP8_MAX, FP8_MAX).astype(
        jnp.bfloat16
    )
    grads_all = lax.all_gather(grads_q, "tensor", axis=1, tiled=True)
    product = lax.dot_general(
        acts_q, grads_all, (((0,), (0,)), ((), ())), preferred_element_type=jnp.float32
    )
    summed = lax.psum_scatter(
        (product / denom).astype(jnp.bfloat16), "dp", scatter_dimension=0, tiled=True
    )
    return summed[None]


def body(observed, section_of, hist_len, roll_index, history, acts, grads):
    section = lax.axis_index("section")
    kinds = hist_len.shape[0]
    total_tensors = history.shape[1]
    slot_count = history.shape[0]
    kind_len = jnp.tile(hist_len, total_tensors // kinds)
    slots = lax.broadcasted_iota(jnp.int32, (slot_count, 1), 0)
    age = (roll_index - slots) % slot_count
    first = jnp.sum((section_of < section).astype(jnp.int32))
    columns = lax.dynamic_slice_in_dim(history, first * kinds, 2, 1)
    pair_len = hist_len[:2]
    old_window = (age >= 1) & (age <= pair_len[None, :])
    old_scale = FP8_MAX / jnp.max(jnp.where(old_window, columns, jnp.float32(0.0)), axis=0)
    owned = jnp.repeat(section_of == section, kinds)
    local = jnp.where(owned, observed.reshape(total_tensors), jnp.float32(0.0))
    merged = merge_amax(local)
    wgrad = weight_grad(acts, grads, old_scale[0], old_scale[1])
    new_history = jnp.where(slots == roll_index, merged[None, :], history)
    new_window = age < kind_len[None, :]
    new_scale = FP8_MAX / jnp.max(jnp.where(new_window, new_history, jnp.float32(0.0)), axis=0)
    return (new_history, new_scale, wgrad)


def solution(mesh):
    in_specs = (
        P("dp", "section", "tensor", None),
        P(),
        P(),
        P(),
        P(),
        P("section", "dp", "tensor"),
        P("section", "dp", "tensor"),
    )
    out_specs = (P(), P(), P("section", ("tensor", "dp"), None))
    return jax.shard_map(body, mesh=mesh, in_specs=in_specs, out_specs=out_specs, check_vma=False)
```

profile of v0, /device:TPU:1, one launch (start us, length us, event | category | flops | bytes accessed | tf_op | source)
XLA Modules:
  0.0 122.2 jit_solution(12922742336281192124)
XLA Ops:
  7.2 0.0 reduce-scatter.2.cloned.1.call-start
  7.9 1.3 %fusion.7 = s32[]{:T(128)} fusion(s32[126]{0:T(128)} %param.8, s32[]{:T(128)S(6)} %axis_index.15), kind=kLoop, calls=%fused_computation.18 | loop fusion | flops 377 | bytes 512 | tf_op jit(solution)/shard_map/reduce_sum | solution.py:39
  9.8 0.9 fusion.6
  10.7 0.6 fusion.11
  12.6 1.6 %clamp_convert_fusion.1 = bf16[1,384,256]{2,1,0:T(8,128)(2,1)S(1)} fusion(bf16[1,384,256]{2,1,0:T(8,128)(2,1)} %param.13, f32[]{:T(128)} %bitcast.2), kind=kLoop, calls=%fused_computation.9 | loop fusion | flops 393216 | bytes 393220 | tf_op jit(solution)/shard_map/convert_element_type | solution.py:18
  14.3 18.0 %all-gather = bf16[1,384,1024]{2,1,0:T(8,128)(2,1)S(1)} all-gather(bf16[1,384,256]{2,1,0:T(8,128)(2,1)S(1)} %clamp_convert_fusion.1), channel_id=2, replica_groups=mesh['dp'=4,'section'=2,'tensor'=4] {'tensor'}, dimensions={2}, use_global_device_ids=true | all-gather | bytes 983040 | tf_op jit(solution)/shard_map/all_gather | solution.py:21
  32.3 9.5 %divide_convert_fusion = bf16[4096,1024]{1,0:T(8,128)(2,1)} fusion(f32[]{:T(128)S(6)} %mul.25, bf16[1,384,4096]{2,1,0:T(8,128)(2,1)} %param.12, f32[]{:T(128)} %bitcast, bf16[1,384,1024]{2,1,0:T(8,128)(2,1)S(1)} %all-gather), kind=kOutput, calls=%fused_computation | convolution fusion | flops 3235905536 | bytes 12320776 | tf_op jit(solution)/shard_map/dot_general | solution.py:22
  41.7 0.0 copy-start.3
  41.8 0.0 copy-start.2
  41.8 0.0 copy-start.1
  41.8 0.0 copy-start
  41.8 0.0 reduce-scatter.2.cloned.1.call-update
  41.8 0.6 copy-done.3
  42.4 0.1 broadcast_in_dim.37
  42.5 0.2 reshape.60
  42.7 0.0 copy-done.2
  42.7 0.2 lt.30
  42.9 0.0 copy-done.1
  43.0 14.9 %pmax.21 = f32[2646]{0:T(1024)S(1)} all-reduce(f32[2646]{0:T(1024)S(1)} %broadcast_select_fusion.1), channel_id=1, replica_groups=mesh['dp'=4,'section'=2,'tensor'=4] {'tensor'}, use_global_device_ids=true, to_apply=%region_0.1 | all-reduce | flops 2646 | bytes 21168 | tf_op jit(solution)/shard_map/pmax | solution.py:10
  57.9 6.1 %pmax.22 = f32[2646]{0:T(1024)S(1)} all-reduce(f32[2646]{0:T(1024)S(1)} %pmax.21), channel_id=1, replica_groups=mesh['dp'=4,'section'=2,'tensor'=4] {'section'}, use_global_device_ids=true, to_apply=%region_1.2 | all-reduce | flops 2646 | bytes 21168 | tf_op jit(solution)/shard_map/pmax | solution.py:11
  64.0 17.9 %pmax.23 = f32[2646]{0:T(1024)S(1)} all-reduce(f32[2646]{0:T(1024)S(1)} %pmax.22), channel_id=1, replica_groups=mesh['dp'=4,'section'=2,'tensor'=4] {'dp'}, use_global_device_ids=true, to_apply=%region_2.3 | all-reduce | flops 2646 | bytes 21168 | tf_op jit(solution)/shard_map/pmax | solution.py:12
  81.8 0.0 copy-done
  81.8 2.9 %select_reduce_fusion = (f32[2646]{0:T(1024)S(1)}, f32[128,2646]{0,1:T(8,128)}) fusion(s32[128]{0:T(128)S(1)} %and_select_fusion.1, s32[2646]{0:T(1024)S(1)} %lt.30, f32[128,2646]{0,1:T(8,128)S(1)} %copy-done, f32[2646]{0:T(1024)S(1)} %pmax.23, pred[128]{0:T(512)(128)(4,1)S(1)} %iota_compare_fusion), kind=kLoop, calls=%fused_computation.6 | loop fusion | flops 1352106 | bytes 2741896 | tf_op jit(solution)/shard_map/reduce_max | solution.py:50
  84.7 0.6 broadcast_divide_fusion
  85.3 30.1 %reduce-scatter.2.cloned.1.call-done = bf16[1024,1024]{1,0:T(8,128)(2,1)} async-done(((bf16[4096,1024]{1,0:T(8,128)(2,1)}), bf16[1024,1024]{1,0:T(8,128)(2,1)}) %reduce-scatter.2.cloned.1.call-update) | async-done | bytes 2097168 | tf_op jit(solution)/shard_map/reduce_scatter | solution.py:25
  (8 shorter events, 0.1 us)
Async XLA Ops:
  7.2 108.2 %reduce-scatter.2.cloned.1.call-start = ((), (), s32[]{:S(2)}) async-start(), calls=%async_computation.1 | async-start | bytes 10485760 | tf_op jit(solution)/shard_map/reduce_scatter | solution.py:25
  41.7 0.7 copy-start.3
  41.8 1.0 copy-start.2
  41.8 1.2 copy-start.1
  41.8 40.1 %copy-start = (f32[128,2646]{0,1:T(8,128)S(1)}, f32[128,2646]{0,1:T(8,128)}, u32[]{:S(2)}) copy-start(f32[128,2646]{0,1:T(8,128)} %param.11) | copy-start | bytes 4064260
Sparse Core Ops, SparseCore 0:
  41.9 73.4 reduce-scatter.1
where the time goes:
time: 123 us; the launch traced here: 122 us
  blocking collectives  56.8 us (46%)
  waiting for transfers between devices  30.1 us (24%)
  between operations  16.7 us (14%)
  matrix products  9.46 us (8%)
  other arithmetic  7.36 us (6%)
  local copies, waits for them, and re-layouts  1.72 us (1%)
    reduce_scatter x1, waiting for transfers between devices, weight_grad(): lax.psum_scatter((product / denom).astype(jnp.bfloat16), 'dp', scatter_di...  30.1 us
    all_gather x1, blocking collectives, weight_grad(): grads_all = lax.all_gather(grads_q, 'tensor', axis=1, tiled=True)  18 us
    pmax x1, blocking collectives, merge_amax(): return lax.pmax(merged, 'dp')  17.9 us
    pmax x1, blocking collectives, merge_amax(): merged = lax.pmax(local, 'tensor')  14.9 us
    dot_general x1, matrix products, weight_grad(): lax.dot_general(acts_q, grads_all, (((0,), (0,)), ((), ())), preferred_el...  9.46 us
    pmax x1, blocking collectives, merge_amax(): merged = lax.pmax(merged, 'section')  6.07 us
    reduce_max x1, other arithmetic, body(): jnp.max(jnp.where(new_window, new_history, jnp.float32(0.0)), axis=0)  2.87 us
  transfers between devices with their start and end apart: 1, of which 1 were waited for; matrix products, arithmetic and copies ran while one was open for 3% of the time, Pallas kernels for 0%

commit v1 on v0

v1 whole, which is shorter than its diff:
```python
import functools

import jax
import jax.numpy as jnp
from jax import lax
from jax.experimental import pallas as pl
from jax.experimental.pallas import tpu as pltpu
from jax.sharding import PartitionSpec as P

FP8_MAX = 448.0
MESH = pl.DeviceIdType.MESH
LANES = 128


def quantize(values, scale):
    return jnp.clip(values.astype(jnp.float32) * scale, -FP8_MAX, FP8_MAX).astype(jnp.bfloat16)


def kernel(
    ndp, nsec, nt, cw,
    roll_ref, len_ref, sec_ref, obs_ref, hist_ref, acts_ref, grads_ref,
    nh_ref, ns_ref, w_ref,
    abuf, gbuf, gq, acc, obuf, hbuf, hout, pre, mine,
    mxbuf, m1buf, mcbuf, m2buf, mzbuf,
    local_sem, ap_sem, a_send, a_recv, gx_send, gx_recv, gz_send, gz_recv, gc_send, gc_recv,
    mx_send, mx_recv, mc_send, mc_recv, mz_send, mz_recv,
):
    d = lax.axis_index("dp")
    s = lax.axis_index("section")
    t = lax.axis_index("tensor")
    core = lax.rem(d, 2)
    pair = d // 2
    partner = d + 1 - 2 * core
    npair = ndp // 2
    T, cols = acts_ref.shape
    w = cols // ndp
    nq = w // cw
    gw = grads_ref.shape[1]
    slots, LT = hist_ref.shape
    kinds = len_ref.shape[0]

    def dev(dp=None, section=None, tensor=None):
        return {
            "dp": d if dp is None else dp,
            "section": s if section is None else section,
            "tensor": t if tensor is None else tensor,
        }

    other_pairs = [lax.rem(pair + j, npair) for j in range(1, npair)]
    other_t = [lax.rem(t + j, nt) for j in range(1, nt)]
    others_sc = []
    for k in range(nsec):
        for c in range(2):
            if k == 0 and c == 0:
                continue
            sec = lax.rem(s + k, nsec)
            dp = 2 * pair + lax.rem(core + c, 2)
            others_sc.append((sec, dp))

    barrier = pltpu.get_barrier_semaphore()
    count = 0
    for p in other_pairs:
        for c in range(2):
            pl.semaphore_signal(barrier, inc=1, device_id=dev(dp=2 * p + c), device_id_type=MESH)
            count += 1
    for tt in other_t:
        pl.semaphore_signal(barrier, inc=1, device_id=dev(tensor=tt), device_id_type=MESH)
        count += 1
    for sec, dp in others_sc:
        pl.semaphore_signal(
            barrier, inc=1, device_id=dev(dp=dp, section=sec), device_id_type=MESH
        )
        count += 1

    own_rows = pl.ds(pl.multiple_of(d * T, T), T)
    load_hist = pltpu.make_async_copy(hist_ref, hbuf, local_sem.at[0])
    load_hist.start()
    load_acts = pltpu.make_async_copy(
        acts_ref.at[:, pl.ds(pl.multiple_of(d * w, w), w)], abuf.at[own_rows, :], local_sem.at[1]
    )
    load_acts.start()
    load_grads = pltpu.make_async_copy(grads_ref, gbuf.at[t, own_rows, :], local_sem.at[2])
    load_grads.start()

    pl.semaphore_wait(barrier, count)

    sends = []

    def send(src, dst, ssem, rsem, device):
        copy = pltpu.make_async_remote_copy(
            src_ref=src, dst_ref=dst, send_sem=ssem, recv_sem=rsem,
            device_id=device, device_id_type=MESH,
        )
        copy.start()
        sends.append(copy)

    def arrived(dst, ssem, rsem):
        pltpu.make_async_remote_copy(
            src_ref=dst, dst_ref=dst, send_sem=ssem, recv_sem=rsem,
            device_id=dev(dp=partner), device_id_type=MESH,
        ).wait_recv()

    def shard(dp, tt):
        return gbuf.at[tt, pl.ds(pl.multiple_of(dp * T, T), T), :]

    for p in other_pairs:
        send(obs_ref, mxbuf.at[pair], mx_send.at[p], mx_recv.at[pair], dev(dp=2 * p + core))
        send(grads_ref, shard(d, t), gx_send.at[p], gx_recv.at[pair], dev(dp=2 * p + core))
    for tt in other_t:
        send(grads_ref, shard(d, t), gz_send.at[pair, tt], gz_recv.at[pair, t], dev(tensor=tt))
    send(grads_ref, shard(d, t), gc_send.at[pair, t], gc_recv.at[pair, t], dev(dp=partner))
    send(
        acts_ref.at[:, pl.ds(pl.multiple_of(partner * w, w), w)], abuf.at[own_rows, :],
        ap_sem.at[0], ap_sem.at[1], dev(dp=partner),
    )
    for q in range(nq):
        for p in other_pairs:
            for c in range(2):
                dest = 2 * p + c
                send(
                    acts_ref.at[:, pl.ds(pl.multiple_of(dest * w + q * cw, cw), cw)],
                    abuf.at[own_rows, pl.ds(q * cw, cw)],
                    a_send.at[q, dest], a_recv.at[q, d], dev(dp=dest),
                )

    layers = sec_ref[...]
    first = jnp.sum((layers < s).astype(jnp.int32), axis=1, keepdims=True) * kinds
    last = jnp.sum((layers <= s).astype(jnp.int32), axis=1, keepdims=True) * kinds
    column = lax.broadcasted_iota(jnp.int32, (1, LT), 1)
    owned = (column >= first) & (column < last)

    for p in other_pairs:
        arrived(mxbuf.at[p], mx_send.at[p], mx_recv.at[p])
    merged = obs_ref[...]
    for p in other_pairs:
        merged = jnp.maximum(merged, mxbuf[p])
    m1buf[...] = jnp.where(owned, merged, 0.0)
    for k, (sec, dp) in enumerate(others_sc):
        send(
            m1buf, mcbuf.at[2 * s + core], mc_send.at[k], mc_recv.at[2 * s + core],
            dev(dp=dp, section=sec),
        )

    for p in other_pairs:
        e = 2 * p + core
        arrived(shard(e, t), gx_send.at[p], gx_recv.at[p])
        for tt in other_t:
            send(shard(e, t), shard(e, t), gz_send.at[p, tt], gz_recv.at[p, t], dev(tensor=tt))
        send(shard(e, t), shard(e, t), gc_send.at[p, t], gc_recv.at[p, t], dev(dp=partner))

    for sec, dp in others_sc:
        slot = 2 * sec + lax.rem(dp, 2)
        arrived(mcbuf.at[slot], mc_send.at[0], mc_recv.at[slot])
    merged = m1buf[...]
    for sec, dp in others_sc:
        merged = jnp.maximum(merged, mcbuf[2 * sec + lax.rem(dp, 2)])
    m2buf[...] = merged
    for tt in other_t:
        send(m2buf, mzbuf.at[t], mz_send.at[tt], mz_recv.at[t], dev(tensor=tt))

    load_hist.wait()
    roll = roll_ref[0]
    slot_id = lax.broadcasted_iota(jnp.int32, (slots, 1), 0)
    age = roll - slot_id
    age = jnp.where(age < 0, age + slots, age)
    best_x = jnp.zeros((1, 1), jnp.float32)
    best_g = jnp.zeros((1, 1), jnp.float32)
    in_x = (age >= 1) & (age <= len_ref[0])
    in_g = (age >= 1) & (age <= len_ref[1])
    blocks = [(b, min(b + LANES, LT)) for b in range(0, LT, LANES)]
    for lo, hi in blocks:
        h = hbuf[:, lo:hi]
        col = lo + lax.broadcasted_iota(jnp.int32, (1, hi - lo), 1)
        group = jnp.floor((col.astype(jnp.float32) + 0.5) * (1.0 / kinds)).astype(jnp.int32)
        kind = col - group * kinds
        length = jnp.zeros((1, hi - lo), jnp.int32)
        for i in range(kinds):
            length = jnp.where(kind == i, len_ref[i], length)
        window = (age >= 1) & (age < length)
        pre[:, lo:hi] = jnp.max(jnp.where(window, h, 0.0), axis=0, keepdims=True)
        hx = jnp.max(jnp.where(in_x, h, 0.0), axis=0, keepdims=True)
        hg = jnp.max(jnp.where(in_g, h, 0.0), axis=0, keepdims=True)
        best_x = jnp.maximum(
            best_x, jnp.max(jnp.where(col == first, hx, 0.0), axis=1, keepdims=True)
        )
        best_g = jnp.maximum(
            best_g, jnp.max(jnp.where(col == first + 1, hg, 0.0), axis=1, keepdims=True)
        )
    sx = FP8_MAX / best_x
    sg = FP8_MAX / best_g
    inverse = 1.0 / (sx * sg)

    load_grads.wait()
    for p in [pair] + other_pairs:
        e = 2 * p + core
        for tt in other_t:
            arrived(shard(e, tt), gz_send.at[p, tt], gz_recv.at[p, tt])
            send(shard(e, tt), shard(e, tt), gc_send.at[p, tt], gc_recv.at[p, tt], dev(dp=partner))

    for tt in other_t:
        arrived(mzbuf.at[tt], mz_send.at[tt], mz_recv.at[tt])
    merged = m2buf[...]
    for tt in other_t:
        merged = jnp.maximum(merged, mzbuf[tt])
    mine[...] = merged
    ns_ref[...] = FP8_MAX / jnp.maximum(pre[...], merged)
    for lo, hi in blocks:
        hout[:, lo:hi] = jnp.where(slot_id == roll, mine[:, lo:hi], hbuf[:, lo:hi])
    store_hist = pltpu.make_async_copy(hout, nh_ref, local_sem.at[3])
    store_hist.start()

    for p in [pair] + other_pairs:
        for tt in range(nt):
            arrived(shard(2 * p + 1 - core, tt), gc_send.at[p, tt], gc_recv.at[p, tt])

    def rows_of(p):
        return pl.ds(pl.multiple_of(p * 2 * T, 2 * T), 2 * T)

    for p in [pair] + other_pairs:
        for tt in range(nt):
            gq[rows_of(p), tt * gw:(tt + 1) * gw] = quantize(gbuf[tt, rows_of(p), :], sg)

    def product(p, q):
        a = quantize(abuf[rows_of(p), q * cw:(q + 1) * cw], sx)
        return lax.dot_general(
            a, gq[rows_of(p), :], (((0,), (0,)), ((), ())), preferred_element_type=jnp.float32
        )

    load_acts.wait()
    arrived(abuf.at[pl.ds(pl.multiple_of(partner * T, T), T), :], ap_sem.at[0], ap_sem.at[1])
    for q in range(nq):
        acc[q * cw:(q + 1) * cw, :] = product(pair, q)
    stores = []
    for q in range(nq):
        span = slice(q * cw, (q + 1) * cw)
        for j, p in enumerate(other_pairs):
            for c in range(2):
                src = 2 * p + c
                arrived(
                    abuf.at[pl.ds(pl.multiple_of(src * T, T), T), pl.ds(q * cw, cw)],
                    a_send.at[q, src], a_recv.at[q, src],
                )
            acc[span, :] += product(p, q)
        obuf[span, :] = (acc[span, :] * inverse).astype(jnp.bfloat16)
        store = pltpu.make_async_copy(obuf.at[span, :], w_ref.at[span, :], local_sem.at[4 + q])
        store.start()
        stores.append(store)
    store_hist.wait()
    for copy in sends:
        copy.wait_send()
    for store in stores:
        store.wait()


def solution(mesh):
    ndp, nsec, nt = mesh.shape["dp"], mesh.shape["section"], mesh.shape["tensor"]

    def body(observed, section_of, hist_len, roll_index, history, acts, grads):
        slots, LT = history.shape
        T, cols = acts.shape[1:]
        gw = grads.shape[2]
        w = cols // ndp
        cw = min(w, 256)
        nq = w // cw
        npair = ndp // 2
        kv = gw * nt
        f32, bf16 = jnp.float32, jnp.bfloat16
        dma = pltpu.SemaphoreType.DMA
        any_spec = pl.BlockSpec(memory_space=pl.ANY)
        vmem = pl.BlockSpec(memory_space=pltpu.VMEM)
        smem = pl.BlockSpec(memory_space=pltpu.SMEM)
        new_history, new_scale, wgrad = pl.pallas_call(
            functools.partial(kernel, ndp, nsec, nt, cw),
            out_shape=(
                jax.ShapeDtypeStruct((slots, LT), f32),
                jax.ShapeDtypeStruct((1, LT), f32),
                jax.ShapeDtypeStruct((w, kv), bf16),
            ),
            in_specs=[smem, smem, vmem, vmem, any_spec, any_spec, any_spec],
            out_specs=(any_spec, vmem, any_spec),
            scratch_shapes=[
                pltpu.VMEM((ndp * T, w), bf16),
                pltpu.VMEM((nt, ndp * T, gw), bf16),
                pltpu.VMEM((ndp * T, kv), bf16),
                pltpu.VMEM((w, kv), f32),
                pltpu.VMEM((w, kv), bf16),
                pltpu.VMEM((slots, LT), f32),
                pltpu.VMEM((slots, LT), f32),
                pltpu.VMEM((1, LT), f32),
                pltpu.VMEM((1, LT), f32),
                pltpu.VMEM((npair, 1, LT), f32),
                pltpu.VMEM((1, LT), f32),
                pltpu.VMEM((2 * nsec, 1, LT), f32),
                pltpu.VMEM((1, LT), f32),
                pltpu.VMEM((nt, 1, LT), f32),
                dma((4 + nq,)),
                dma((2,)),
                dma((nq, ndp)),
                dma((nq, ndp)),
                dma((npair,)),
                dma((npair,)),
                dma((npair, nt)),
                dma((npair, nt)),
                dma((npair, nt)),
                dma((npair, nt)),
                dma((npair,)),
                dma((npair,)),
                dma((2 * nsec,)),
                dma((2 * nsec,)),
                dma((nt,)),
                dma((nt,)),
            ],
            compiler_params=pltpu.CompilerParams(
                collective_id=0, has_side_effects=True, vmem_limit_bytes=60 * 1024 * 1024
            ),
            name="merge_and_grad",
        )(
            roll_index.reshape(1), hist_len, section_of.reshape(1, -1),
            observed.reshape(1, LT), history, acts[0], grads[0],
        )
        return new_history, new_scale.reshape(LT), wgrad[None]

    in_specs = (
        P("dp", "section", "tensor", None),
        P(),
        P(),
        P(),
        P(),
        P("section", "dp", "tensor"),
        P("section", "dp", "tensor"),
    )
    out_specs = (P(), P(), P("section", ("tensor", "dp"), None))
    return jax.shard_map(body, mesh=mesh, in_specs=in_specs, out_specs=out_specs, check_vma=False)
```

time: 123 us -> 58.9 us (0.48)
  the two profiles are of different devices: /device:TPU:1 before, /device:TPU:0 now
where the time goes in v1:
time: 58.9 us; the launch traced here: 58.7 us
  Pallas kernels  49.6 us (84%)
  local copies, waits for them, and re-layouts  7.16 us (12%)
  between operations  1.3 us (2%)
  other arithmetic  0.63 us (1%)
    pallas_call x1, Pallas kernels, body(): pl.pallas_call(functools.partial(kernel, ndp, nsec, nt, cw), out_shape=(j...  49.6 us
    unnamed x7, local copies, waits for them, and re-layouts  7.16 us

profile of v1, /device:TPU:0, one launch (start us, length us, event | category | flops | bytes accessed | tf_op | source)
XLA Modules:
  0.0 58.7 jit_solution(2601009665981797914)
XLA Ops:
  1.3 2.8 %copy.10.hist_ref = f32[128,2646]{1,0:T(8,128)} copy(f32[128,2646]{0,1:T(8,128)} %param.11) | data formatting | bytes 2709504 | tf_op args[4]
  4.1 49.6 %merge_and_grad.1 = (f32[128,2646]{1,0:T(8,128)}, f32[1,2646]{1,0:T(1,128)}, bf16[1024,1024]{1,0:T(8,128)(2,1)}) custom-call(s32[1]{0:T(128)} %bitcast.6.roll_ref, s32[21]{0:T(128)} %len_ref.1, s32[1,126]{1,0:T(1,128)} %bitcast.11, f32[1,2646]{1,0:T(1,128)} %bitcast.10, f32[128,2646]{1,0:T(8,128)} %copy.10.hist_ref, bf16[384,4096]{1,0:T(8,128)(2,1)} %bitcast.7, ...), custom_call_target="tpu_custom_call" | custom-call | tf_op jit(solution)/shard_map/merge_and_grad/pallas_call | solution.py:272
  53.7 0.0 copy-start.1
  53.7 0.0 copy-start
  53.7 3.0 %copy.11 = f32[128,2646]{0,1:T(8,128)} copy(f32[128,2646]{1,0:T(8,128)} %get-tuple-element.9) | data formatting | bytes 2709504
  56.7 0.0 copy-done.1
  56.7 0.6 %reduce = f32[2646]{0:T(1024)} reduce(f32[1,2646]{1,0:T(1,128)S(1)} %copy-done.1, f32[]{:T(128)} %constant.3), dimensions={0}, to_apply=%get-tuple-element.7.reduce_sub_computation | reduce | bytes 21172 | tf_op jit(solution)/shard_map/merge_and_grad/pallas_call | solution.py:272
  57.4 0.0 copy-done
  57.4 1.3 %copy.14 = bf16[1,1024,1024]{2,1,0:T(8,128)(2,1)} copy(bf16[1,1024,1024]{2,1,0:T(8,128)(2,1)S(1)} %bitcast.8) | data formatting | bytes 4194304
Async XLA Ops:
  53.7 3.0 %copy-start.1 = (f32[1,2646]{1,0:T(1,128)S(1)}, f32[1,2646]{1,0:T(1,128)}, u32[]{:S(2)}) copy-start(f32[1,2646]{1,0:T(1,128)} %get-tuple-element.7) | copy-start | bytes 31756
  53.7 3.6 %copy-start = (bf16[1024,1024]{1,0:T(8,128)(2,1)S(1)}, bf16[1024,1024]{1,0:T(8,128)(2,1)}, u32[]{:S(2)}) copy-start(bf16[1024,1024]{1,0:T(8,128)(2,1)} %get-tuple-element.8) | copy-start | bytes 6291460

commit v2 on v1

--- a/solution.py
+++ b/solution.py
@@ -22,7 +22,7 @@
     nh_ref, ns_ref, w_ref,
     abuf, gbuf, gq, acc, obuf, hbuf, hout, pre, mine,
     mxbuf, m1buf, mcbuf, m2buf, mzbuf,
-    local_sem, ap_sem, a_send, a_recv, gx_send, gx_recv, gz_send, gz_recv, gc_send, gc_recv,
+    local_sem, ap_sem, a_send, a_recv, gx_send, gx_recv, gr_send, gl_send, gz_recv, gc_send, gc_recv,
     mx_send, mx_recv, mc_send, mc_recv, mz_send, mz_recv,
 ):
     d = lax.axis_index("dp")
@@ -36,7 +36,7 @@
     w = cols // ndp
     nq = w // cw
     gw = grads_ref.shape[1]
-    slots, LT = hist_ref.shape
+    LT, slots = hist_ref.shape
     kinds = len_ref.shape[0]
 
     def dev(dp=None, section=None, tensor=None):
@@ -73,7 +73,7 @@
         count += 1
 
     own_rows = pl.ds(pl.multiple_of(d * T, T), T)
-    load_hist = pltpu.make_async_copy(hist_ref, hbuf, local_sem.at[0])
+    load_hist = pltpu.make_async_copy(hist_ref, hbuf.at[pl.ds(0, LT), :], local_sem.at[0])
     load_hist.start()
     load_acts = pltpu.make_async_copy(
         acts_ref.at[:, pl.ds(pl.multiple_of(d * w, w), w)], abuf.at[own_rows, :], local_sem.at[1]
@@ -106,8 +106,46 @@
     for p in other_pairs:
         send(obs_ref, mxbuf.at[pair], mx_send.at[p], mx_recv.at[pair], dev(dp=2 * p + core))
         send(grads_ref, shard(d, t), gx_send.at[p], gx_recv.at[pair], dev(dp=2 * p + core))
-    for tt in other_t:
-        send(grads_ref, shard(d, t), gz_send.at[pair, tt], gz_recv.at[pair, t], dev(tensor=tt))
+    def along(src, p, origin, right):
+        here = shard(2 * p + core, origin)
+        ssem = (gr_send if right else gl_send).at[p, origin]
+        there = t + 1 if right else t - 1
+        return pltpu.make_async_remote_copy(
+            src_ref=here if src is None else src, dst_ref=here, send_sem=ssem,
+            recv_sem=gz_recv.at[p, origin],
+            device_id=dev(tensor=there), device_id_type=MESH,
+        )
+
+    passed = []
+
+    def pass_on(src, p, origin, right, has_origin):
+        cond = has_origin & ((t < nt - 1) if right else (t > 0))
+        pl.when(cond)(lambda: along(src, p, origin, right).start())
+        passed.append((cond, src, p, origin, right))
+
+    def to_core(p, origin):
+        here = shard(2 * p + core, origin)
+        return pltpu.make_async_remote_copy(
+            src_ref=here, dst_ref=here, send_sem=gc_send.at[p, origin],
+            recv_sem=gc_recv.at[p, origin], device_id=dev(dp=partner), device_id_type=MESH,
+        )
+
+    def relay(p, k):
+        for right in (True, False):
+            origin = t - k if right else t + k
+            has = (origin >= 0) if right else (origin < nt)
+
+            @pl.when(has)
+            def take():
+                along(None, p, origin, right).wait_recv()
+                to_core(p, origin).start()
+
+            if k < nt - 1:
+                pass_on(None, p, origin, right, has)
+
+    always = t >= 0
+    pass_on(grads_ref, pair, t, True, always)
+    pass_on(grads_ref, pair, t, False, always)
     send(grads_ref, shard(d, t), gc_send.at[pair, t], gc_recv.at[pair, t], dev(dp=partner))
     send(
         acts_ref.at[:, pl.ds(pl.multiple_of(partner * w, w), w)], abuf.at[own_rows, :],
@@ -141,12 +179,16 @@
             dev(dp=dp, section=sec),
         )
 
-    for p in other_pairs:
-        e = 2 * p + core
-        arrived(shard(e, t), gx_send.at[p], gx_recv.at[p])
-        for tt in other_t:
-            send(shard(e, t), shard(e, t), gz_send.at[p, tt], gz_recv.at[p, t], dev(tensor=tt))
-        send(shard(e, t), shard(e, t), gc_send.at[p, t], gc_recv.at[p, t], dev(dp=partner))
+    def from_other_pairs(k):
+        for p in other_pairs:
+            if k == 0:
+                e = 2 * p + core
+                arrived(shard(e, t), gx_send.at[p], gx_recv.at[p])
+                pass_on(None, p, t, True, always)
+                pass_on(None, p, t, False, always)
+                send(shard(e, t), shard(e, t), gc_send.at[p, t], gc_recv.at[p, t], dev(dp=partner))
+            else:
+                relay(p, k)
 
     for sec, dp in others_sc:
         slot = 2 * sec + lax.rem(dp, 2)
@@ -161,15 +203,16 @@
     load_hist.wait()
     roll = roll_ref[0]
     slot_id = lax.broadcasted_iota(jnp.int32, (slots, 1), 0)
+    lane_id = lax.broadcasted_iota(jnp.int32, (1, slots), 1)
     age = roll - slot_id
     age = jnp.where(age < 0, age + slots, age)
     best_x = jnp.zeros((1, 1), jnp.float32)
     best_g = jnp.zeros((1, 1), jnp.float32)
     in_x = (age >= 1) & (age <= len_ref[0])
     in_g = (age >= 1) & (age <= len_ref[1])
-    blocks = [(b, min(b + LANES, LT)) for b in range(0, LT, LANES)]
+    blocks = [(b, b + LANES) for b in range(0, LT, LANES)]
     for lo, hi in blocks:
-        h = hbuf[:, lo:hi]
+        h = hbuf[lo:hi, :].T
         col = lo + lax.broadcasted_iota(jnp.int32, (1, hi - lo), 1)
         group = jnp.floor((col.astype(jnp.float32) + 0.5) * (1.0 / kinds)).astype(jnp.int32)
         kind = col - group * kinds
@@ -191,32 +234,30 @@
     inverse = 1.0 / (sx * sg)
 
     load_grads.wait()
-    for p in [pair] + other_pairs:
-        e = 2 * p + core
-        for tt in other_t:
-            arrived(shard(e, tt), gz_send.at[p, tt], gz_recv.at[p, tt])
-            send(shard(e, tt), shard(e, tt), gc_send.at[p, tt], gc_recv.at[p, tt], dev(dp=partner))
+    for k in range(1, nt):
+        relay(pair, k)
+        if k < nt:
+            from_other_pairs(k - 1)
 
     for tt in other_t:
         arrived(mzbuf.at[tt], mz_send.at[tt], mz_recv.at[tt])
     merged = m2buf[...]
     for tt in other_t:
         merged = jnp.maximum(merged, mzbuf[tt])
-    mine[...] = merged
-    ns_ref[...] = FP8_MAX / jnp.maximum(pre[...], merged)
+    mine[:, 0:LT] = merged
+    ns_ref[...] = FP8_MAX / jnp.maximum(pre[:, 0:LT], merged)
     for lo, hi in blocks:
-        hout[:, lo:hi] = jnp.where(slot_id == roll, mine[:, lo:hi], hbuf[:, lo:hi])
-    store_hist = pltpu.make_async_copy(hout, nh_ref, local_sem.at[3])
+        row = jnp.broadcast_to(mine[:, lo:hi], (slots, hi - lo)).T
+        hout[lo:hi, :] = jnp.where(lane_id == roll, row, hbuf[lo:hi, :])
+    store_hist = pltpu.make_async_copy(hout.at[pl.ds(0, LT), :], nh_ref, local_sem.at[3])
     store_hist.start()
 
-    for p in [pair] + other_pairs:
+    def rows_of(p):
+        return pl.ds(pl.multiple_of(p * 2 * T, 2 * T), 2 * T)
+
+    def grads_of(p):
         for tt in range(nt):
             arrived(shard(2 * p + 1 - core, tt), gc_send.at[p, tt], gc_recv.at[p, tt])
-
-    def rows_of(p):
-        return pl.ds(pl.multiple_of(p * 2 * T, 2 * T), 2 * T)
-
-    for p in [pair] + other_pairs:
         for tt in range(nt):
             gq[rows_of(p), tt * gw:(tt + 1) * gw] = quantize(gbuf[tt, rows_of(p), :], sg)
 
@@ -228,8 +269,12 @@
 
     load_acts.wait()
     arrived(abuf.at[pl.ds(pl.multiple_of(partner * T, T), T), :], ap_sem.at[0], ap_sem.at[1])
+    grads_of(pair)
     for q in range(nq):
         acc[q * cw:(q + 1) * cw, :] = product(pair, q)
+    from_other_pairs(nt - 1)
+    for p in other_pairs:
+        grads_of(p)
     stores = []
     for q in range(nq):
         span = slice(q * cw, (q + 1) * cw)
@@ -248,6 +293,12 @@
     store_hist.wait()
     for copy in sends:
         copy.wait_send()
+    for cond, src, p, origin, right in passed:
+        pl.when(cond)(lambda: along(src, p, origin, right).wait_send())
+    for p in [pair] + other_pairs:
+        for k in range(1, nt):
+            for origin, has in ((t - k, t - k >= 0), (t + k, t + k < nt)):
+                pl.when(has)(lambda: to_core(p, origin).wait_send())
     for store in stores:
         store.wait()
 
@@ -264,19 +315,21 @@
         nq = w // cw
         npair = ndp // 2
         kv = gw * nt
+        padded = pl.cdiv(LT, LANES) * LANES
         f32, bf16 = jnp.float32, jnp.bfloat16
         dma = pltpu.SemaphoreType.DMA
+        hbm = pl.BlockSpec(memory_space=pltpu.HBM)
         any_spec = pl.BlockSpec(memory_space=pl.ANY)
         vmem = pl.BlockSpec(memory_space=pltpu.VMEM)
         smem = pl.BlockSpec(memory_space=pltpu.SMEM)
         new_history, new_scale, wgrad = pl.pallas_call(
             functools.partial(kernel, ndp, nsec, nt, cw),
             out_shape=(
-                jax.ShapeDtypeStruct((slots, LT), f32),
+                jax.ShapeDtypeStruct((LT, slots), f32),
                 jax.ShapeDtypeStruct((1, LT), f32),
                 jax.ShapeDtypeStruct((w, kv), bf16),
             ),
-            in_specs=[smem, smem, vmem, vmem, any_spec, any_spec, any_spec],
+            in_specs=[smem, smem, vmem, vmem, hbm, hbm, hbm],
             out_specs=(any_spec, vmem, any_spec),
             scratch_shapes=[
                 pltpu.VMEM((ndp * T, w), bf16),
@@ -284,10 +337,10 @@
                 pltpu.VMEM((ndp * T, kv), bf16),
                 pltpu.VMEM((w, kv), f32),
                 pltpu.VMEM((w, kv), bf16),
-                pltpu.VMEM((slots, LT), f32),
-                pltpu.VMEM((slots, LT), f32),
-                pltpu.VMEM((1, LT), f32),
-                pltpu.VMEM((1, LT), f32),
+                pltpu.VMEM((padded, slots), f32),
+                pltpu.VMEM((padded, slots), f32),
+                pltpu.VMEM((1, padded), f32),
+                pltpu.VMEM((1, padded), f32),
                 pltpu.VMEM((npair, 1, LT), f32),
                 pltpu.VMEM((1, LT), f32),
                 pltpu.VMEM((2 * nsec, 1, LT), f32),
@@ -299,6 +352,7 @@
                 dma((nq, ndp)),
                 dma((npair,)),
                 dma((npair,)),
+                dma((npair, nt)),
                 dma((npair, nt)),
                 dma((npair, nt)),
                 dma((npair, nt)),
@@ -316,9 +370,9 @@
             name="merge_and_grad",
         )(
             roll_index.reshape(1), hist_len, section_of.reshape(1, -1),
-            observed.reshape(1, LT), history, acts[0], grads[0],
-        )
-        return new_history, new_scale.reshape(LT), wgrad[None]
+            observed.reshape(1, LT), history.T, acts[0], grads[0],
+        )
+        return new_history.T, new_scale.reshape(LT), wgrad[None]
 
     in_specs = (
         P("dp", "section", "tensor", None),

time: 58.9 us -> 55.2 us (0.937)
  the two profiles are of different devices: /device:TPU:0 before, /device:TPU:1 now
where the time goes in v2:
time: 55.2 us; the launch traced here: 54.9 us
  Pallas kernels  48.3 us (88%)
  local copies, waits for them, and re-layouts  3.81 us (7%)
  other arithmetic  1.48 us (3%)
  between operations  1.29 us (2%)
    pallas_call x1, Pallas kernels, body(): pl.pallas_call(functools.partial(kernel, ndp, nsec, nt, cw), out_shape=(j...  48.3 us
    unnamed x4, local copies, waits for them, and re-layouts  3.81 us
    pallas_call x1, other arithmetic, body(): pl.pallas_call(functools.partial(kernel, ndp, nsec, nt, cw), out_shape=(j...  1.48 us

profile of v2, /device:TPU:1, one launch (start us, length us, event | category | flops | bytes accessed | tf_op | source)
XLA Modules:
  0.0 54.9 jit_solution(1179288215439376914)
XLA Ops:
  1.3 48.3 %merge_and_grad.1 = (f32[2646,128]{1,0:T(8,128)}, f32[1,2646]{1,0:T(1,128)}, bf16[1024,1024]{1,0:T(8,128)(2,1)}) custom-call(s32[1]{0:T(128)} %bitcast.8.roll_ref, s32[21]{0:T(128)} %len_ref.1, s32[1,126]{1,0:T(1,128)} %bitcast.15, f32[1,2646]{1,0:T(1,128)} %bitcast.14, f32[2646,128]{1,0:T(8,128)} %bitcast.11, bf16[384,4096]{1,0:T(8,128)(2,1)} %bitcast.9, ...), custom_call_target="tpu_custom_call" | custom-call | tf_op jit(solution)/shard_map/merge_and_grad/pallas_call | solution.py:325
  49.6 0.0 copy-start
  49.6 1.5 %reduce = f32[2646]{0:T(1024)} reduce(f32[1,2646]{1,0:T(1,128)} %get-tuple-element.7, f32[]{:T(128)} %constant.3), dimensions={0}, to_apply=%get-tuple-element.7.reduce_sub_computation | reduce | bytes 21172 | tf_op jit(solution)/shard_map/merge_and_grad/pallas_call | solution.py:325
  51.1 2.5 %copy.13 = f32[128,2646]{0,1:T(8,128)} copy(f32[128,2646]{0,1:T(8,128)} %bitcast.12) | data formatting | bytes 2709504
  53.6 0.0 copy-done
  53.6 1.3 %copy.14 = bf16[1,1024,1024]{2,1,0:T(8,128)(2,1)} copy(bf16[1,1024,1024]{2,1,0:T(8,128)(2,1)S(1)} %bitcast.10) | data formatting | bytes 4194304
Async XLA Ops:
  49.6 4.0 %copy-start = (bf16[1024,1024]{1,0:T(8,128)(2,1)S(1)}, bf16[1024,1024]{1,0:T(8,128)(2,1)}, u32[]{:S(2)}) copy-start(bf16[1024,1024]{1,0:T(8,128)(2,1)} %get-tuple-element.8) | copy-start | bytes 6291460

commit v3 on v2

--- a/solution.py
+++ b/solution.py
@@ -301,6 +301,27 @@
                 pl.when(has)(lambda: to_core(p, origin).wait_send())
     for store in stores:
         store.wait()
+
+
+def hand_over(scale_ref, hist_ref, w_ref, ns_ref, nh_ref, wout_ref, hbuf, wbuf, in_sem, out_sem):
+    rows, cut = w_ref.shape[0], hist_ref.shape[0] // 16 * 8
+    step = max(rows // 4, 16)
+    spans = [(w_ref, wbuf, wout_ref, lo, step) for lo in range(0, rows, step)]
+    spans.append((hist_ref, hbuf, nh_ref, 0, cut))
+    spans.append((hist_ref, hbuf, nh_ref, cut, hist_ref.shape[0] - cut))
+    reads, writes = [], []
+    for i, (src, held, dst, lo, n) in enumerate(spans):
+        span = pl.ds(lo, n)
+        reads.append(pltpu.make_async_copy(src.at[span, :], held.at[span, :], in_sem.at[i]))
+        writes.append(pltpu.make_async_copy(held.at[span, :], dst.at[span, :], out_sem.at[i]))
+    for read in reads:
+        read.start()
+    ns_ref[...] = scale_ref[...].reshape(ns_ref.shape)
+    for read, write in zip(reads, writes):
+        read.wait()
+        write.start()
+    for write in writes:
+        write.wait()
 
 
 def solution(mesh):
@@ -372,7 +393,25 @@
             roll_index.reshape(1), hist_len, section_of.reshape(1, -1),
             observed.reshape(1, LT), history.T, acts[0], grads[0],
         )
-        return new_history.T, new_scale.reshape(LT), wgrad[None]
+        new_scale, new_history, wgrad = pl.pallas_call(
+            hand_over,
+            out_shape=(
+                jax.ShapeDtypeStruct((LT,), f32),
+                jax.ShapeDtypeStruct((LT, slots), f32),
+                jax.ShapeDtypeStruct((w, kv), bf16),
+            ),
+            in_specs=[vmem, any_spec, any_spec],
+            out_specs=(vmem, any_spec, any_spec),
+            scratch_shapes=[
+                pltpu.VMEM((LT, slots), f32),
+                pltpu.VMEM((w, kv), bf16),
+                dma((8,)),
+                dma((8,)),
+            ],
+            compiler_params=pltpu.CompilerParams(vmem_limit_bytes=60 * 1024 * 1024),
+            name="hand_over",
+        )(new_scale, new_history, wgrad)
+        return new_history.T, new_scale, wgrad[None]
 
     in_specs = (
         P("dp", "section", "tensor", None),

time: 55.2 us -> 54.2 us (0.982)
  Pallas kernels: 48.3 us -> 52.6 us
  local copies, waits for them, and re-layouts: 3.81 us -> 0 us
  other arithmetic: 1.48 us -> 0 us
    pallas_call x0 -> x1, Pallas kernels: none -> 4.24 us  [body(): pl.pallas_call(hand_over, out_shape=(jax.ShapeDtypeStruct((LT,), f32), ja...]
    unnamed x4 -> x0, local copies, waits for them, and re-layouts: 3.81 us -> none
    pallas_call x1 -> x0, other arithmetic: 1.48 us -> none  [body(): pl.pallas_call(functools.partial(kernel, ndp, nsec, nt, cw), out_shape=(j...]
where the time goes in v3:
time: 54.2 us; the launch traced here: 53.8 us
  Pallas kernels  52.6 us (97%)
  between operations  1.29 us (2%)
    pallas_call x1, Pallas kernels, body(): pl.pallas_call(functools.partial(kernel, ndp, nsec, nt, cw), out_shape=(j...  48.3 us
    pallas_call x1, Pallas kernels, body(): pl.pallas_call(hand_over, out_shape=(jax.ShapeDtypeStruct((LT,), f32), ja...  4.24 us

profile of v3, /device:TPU:1, one launch (start us, length us, event | category | flops | bytes accessed | tf_op | source)
XLA Modules:
  0.0 53.8 jit_solution(13222291892464228794)
XLA Ops:
  1.3 48.3 %merge_and_grad.1 = (f32[2646,128]{1,0:T(8,128)}, f32[1,2646]{1,0:T(1,128)}, bf16[1024,1024]{1,0:T(8,128)(2,1)}) custom-call(s32[1]{0:T(128)} %bitcast.8.roll_ref, s32[21]{0:T(128)} %len_ref.1, s32[1,126]{1,0:T(1,128)} %bitcast.13, f32[1,2646]{1,0:T(1,128)} %bitcast.12, f32[2646,128]{1,0:T(8,128)} %bitcast.10, bf16[384,4096]{1,0:T(8,128)(2,1)} %bitcast.9, ...), custom_call_target="tpu_custom_call" | custom-call | tf_op jit(solution)/shard_map/merge_and_grad/pallas_call | solution.py:346
  49.6 4.2 %hand_over.1 = (f32[2646]{0:T(1024)}, f32[2646,128]{1,0:T(8,128)}, bf16[1024,1024]{1,0:T(8,128)(2,1)}) custom-call(f32[1,2646]{1,0:T(1,128)} %get-tuple-element.9.scale_ref, f32[2646,128]{1,0:T(8,128)} %get-tuple-element.10.hist_ref, bf16[1024,1024]{1,0:T(8,128)(2,1)} %get-tuple-element.11.w_ref), custom_call_target="tpu_custom_call" | custom-call | tf_op jit(solution)/shard_map/hand_over/pallas_call | solution.py:396

commit v4 on v3

--- a/solution.py
+++ b/solution.py
@@ -14,6 +14,13 @@
 
 def quantize(values, scale):
     return jnp.clip(values.astype(jnp.float32) * scale, -FP8_MAX, FP8_MAX).astype(jnp.bfloat16)
+
+
+def chunks(w, cw):
+    spans = [(lo, cw) for lo in range(0, w, cw)]
+    if cw % (2 * LANES) == 0:
+        spans[-1:] = [(w - cw, cw // 2), (w - cw // 2, cw // 2)]
+    return spans
 
 
 def kernel(
@@ -34,7 +41,7 @@
     npair = ndp // 2
     T, cols = acts_ref.shape
     w = cols // ndp
-    nq = w // cw
+    spans = chunks(w, cw)
     gw = grads_ref.shape[1]
     LT, slots = hist_ref.shape
     kinds = len_ref.shape[0]
@@ -151,13 +158,13 @@
         acts_ref.at[:, pl.ds(pl.multiple_of(partner * w, w), w)], abuf.at[own_rows, :],
         ap_sem.at[0], ap_sem.at[1], dev(dp=partner),
     )
-    for q in range(nq):
+    for q, (lo, n) in enumerate(spans):
         for p in other_pairs:
             for c in range(2):
                 dest = 2 * p + c
                 send(
-                    acts_ref.at[:, pl.ds(pl.multiple_of(dest * w + q * cw, cw), cw)],
-                    abuf.at[own_rows, pl.ds(q * cw, cw)],
+                    acts_ref.at[:, pl.ds(pl.multiple_of(dest * w + lo, LANES), n)],
+                    abuf.at[own_rows, pl.ds(lo, n)],
                     a_send.at[q, dest], a_recv.at[q, d], dev(dp=dest),
                 )
 
@@ -261,8 +268,8 @@
         for tt in range(nt):
             gq[rows_of(p), tt * gw:(tt + 1) * gw] = quantize(gbuf[tt, rows_of(p), :], sg)
 
-    def product(p, q):
-        a = quantize(abuf[rows_of(p), q * cw:(q + 1) * cw], sx)
+    def product(p, lo, n):
+        a = quantize(abuf[rows_of(p), lo:lo + n], sx)
         return lax.dot_general(
             a, gq[rows_of(p), :], (((0,), (0,)), ((), ())), preferred_element_type=jnp.float32
         )
@@ -270,22 +277,22 @@
     load_acts.wait()
     arrived(abuf.at[pl.ds(pl.multiple_of(partner * T, T), T), :], ap_sem.at[0], ap_sem.at[1])
     grads_of(pair)
-    for q in range(nq):
-        acc[q * cw:(q + 1) * cw, :] = product(pair, q)
+    for lo in range(0, w, cw):
+        acc[lo:lo + cw, :] = product(pair, lo, cw)
     from_other_pairs(nt - 1)
     for p in other_pairs:
         grads_of(p)
     stores = []
-    for q in range(nq):
-        span = slice(q * cw, (q + 1) * cw)
+    for q, (lo, n) in enumerate(spans):
+        span = slice(lo, lo + n)
         for j, p in enumerate(other_pairs):
             for c in range(2):
                 src = 2 * p + c
                 arrived(
-                    abuf.at[pl.ds(pl.multiple_of(src * T, T), T), pl.ds(q * cw, cw)],
+                    abuf.at[pl.ds(pl.multiple_of(src * T, T), T), pl.ds(lo, n)],
                     a_send.at[q, src], a_recv.at[q, src],
                 )
-            acc[span, :] += product(p, q)
+            acc[span, :] += product(p, lo, n)
         obuf[span, :] = (acc[span, :] * inverse).astype(jnp.bfloat16)
         store = pltpu.make_async_copy(obuf.at[span, :], w_ref.at[span, :], local_sem.at[4 + q])
         store.start()
@@ -333,7 +340,7 @@
         gw = grads.shape[2]
         w = cols // ndp
         cw = min(w, 256)
-        nq = w // cw
+        nq = len(chunks(w, cw))
         npair = ndp // 2
         kv = gw * nt
         padded = pl.cdiv(LT, LANES) * LANES

time: 54.2 us -> 53.9 us (level)
  no operation moved by 1% of the time
where the time goes in v4:
time: 53.9 us; the launch traced here: 53.6 us
  Pallas kernels  52.3 us (97%)
  between operations  1.29 us (2%)
    pallas_call x1, Pallas kernels, body(): pl.pallas_call(functools.partial(kernel, ndp, nsec, nt, cw), out_shape=(j...  48.1 us
    pallas_call x1, Pallas kernels, body(): pl.pallas_call(hand_over, out_shape=(jax.ShapeDtypeStruct((LT,), f32), ja...  4.24 us

profile of v4, /device:TPU:1, one launch (start us, length us, event | category | flops | bytes accessed | tf_op | source)
XLA Modules:
  0.0 53.6 jit_solution(16383647926865216158)
XLA Ops:
  1.3 48.1 %merge_and_grad.1 = (f32[2646,128]{1,0:T(8,128)}, f32[1,2646]{1,0:T(1,128)}, bf16[1024,1024]{1,0:T(8,128)(2,1)}) custom-call(s32[1]{0:T(128)} %bitcast.8.roll_ref, s32[21]{0:T(128)} %len_ref.1, s32[1,126]{1,0:T(1,128)} %bitcast.13, f32[1,2646]{1,0:T(1,128)} %bitcast.12, f32[2646,128]{1,0:T(8,128)} %bitcast.10, bf16[384,4096]{1,0:T(8,128)(2,1)} %bitcast.9, ...), custom_call_target="tpu_custom_call" | custom-call | tf_op jit(solution)/shard_map/merge_and_grad/pallas_call | solution.py:353
  49.4 4.2 %hand_over.1 = (f32[2646]{0:T(1024)}, f32[2646,128]{1,0:T(8,128)}, bf16[1024,1024]{1,0:T(8,128)(2,1)}) custom-call(f32[1,2646]{1,0:T(1,128)} %get-tuple-element.9.scale_ref, f32[2646,128]{1,0:T(8,128)} %get-tuple-element.10.hist_ref, bf16[1024,1024]{1,0:T(8,128)(2,1)} %get-tuple-element.11.w_ref), custom_call_target="tpu_custom_call" | custom-call | tf_op jit(solution)/shard_map/hand_over/pallas_call | solution.py:403
